TPU v7x, 32 devices: a whole 2x2x4 slice. The times are simulated.
32 devices in a mesh: table: 8 (over y, x, core), batch: 4 (over z).
Axes of the slice: x: 2, y: 2, z: 4, core: 2. Of those that a mesh axis runs over, the one named last changes fastest.
Arguments:
- queries: bfloat16 [128, 4, 512], P(('table', 'batch')), may hold values from -5 to 5
- indices: int32 [128, 4, 32], P(('table', 'batch')), may hold values from 0 to 262143, as said below
- first_keys: bfloat16 [4, 256, 256], P(None, ('table', 'batch')), may hold values from -4 to 4
- second_keys: bfloat16 [4, 1024, 256], replicated, may hold values from -4 to 4
- values: bfloat16 [262144, 1024], P(('table', 'batch')), may hold values from -6 to 6
Outputs:
- memory_read: bfloat16 [128, 1024], P(('table', 'batch'))
Inputs may be any that keep to these rules, and one draw needn't show every extreme that they name: `indices`: row r of the value table belongs to device r // 8192 of table+batch. The entries of the 4 sequences of one device name rows of any one owner at most 32 times, and one owner is named exactly 32 times by the entries of every device.
All inputs are finite; a program needn't handle non-finite values.
Results may differ from a plain program's by a relative error of at most 0.005.
Values may be sent and summed in bfloat16 or wider, within the bound.
A program may use at most 64 MiB of HBM per device.

v0:
```python
import jax
import jax.numpy as jnp
from jax import lax
from jax.sharding import PartitionSpec as P


def decode_codes(codes, head_count, table_rows):
    usable = codes >= 0
    local_row = jnp.where(usable, codes % table_rows, -1)
    head_ids = jnp.where(usable, codes // table_rows % head_count, 0)
    seq_local = jnp.where(usable, codes // (table_rows * head_count), -1)
    return (usable, local_row, head_ids, seq_local)


def answer_slots(request_pair, first_keys, values):
    query_first, codes = request_pair
    head_count, first_count, half_width = first_keys.shape
    table_rows = values.shape[0]
    sub_count = table_rows // first_count
    usable, local_row, head_ids, seq_local = decode_codes(codes, head_count, table_rows)
    key_slot = jnp.where(usable, head_ids * first_count + local_row // sub_count, -1)
    key_pick = (
        key_slot[..., None] == jnp.arange(head_count * first_count, dtype=jnp.int32)
    ).astype(jnp.bfloat16)
    key_rows = jnp.einsum(
        "dnc,ck->dnk",
        key_pick,
        first_keys.reshape(head_count * first_count, half_width),
        preferred_element_type=jnp.float32,
    )
    first_part = jnp.sum(query_first.astype(jnp.float32) * key_rows, axis=-1)
    row_pick = (local_row[..., None] == jnp.arange(table_rows, dtype=jnp.int32)).astype(
        jnp.bfloat16
    )
    fetched = jnp.einsum(
        "dnv,vc->dnc", row_pick, values, preferred_element_type=jnp.float32
    ).astype(jnp.bfloat16)
    return (first_part, fetched, seq_local)


def second_scores(query_second, head_ids, columns, second_keys):
    head_count, sub_count, half_width = second_keys.shape
    key_table = second_keys.reshape(head_count * sub_count, half_width)
    where_rows = jnp.clip(head_ids * sub_count + columns, 0, head_count * sub_count - 1)
    key_rows = jnp.take(key_table, where_rows, axis=0)
    return jnp.sum(query_second.astype(jnp.float32) * key_rows.astype(jnp.float32), axis=-1)


def combine_home(weights, fetched, seq_local, seqs_dev):
    seq_ids = jnp.arange(seqs_dev, dtype=jnp.int32)
    mixing = jnp.where(
        seq_local[:, None, :] == seq_ids[None, :, None],
        weights[:, None, :],
        jnp.zeros((), jnp.bfloat16),
    )
    owner_part = jnp.einsum("dsc,dcv->dsv", mixing, fetched, preferred_element_type=jnp.float32)
    arrived = lax.all_to_all(
        owner_part, ("table", "batch"), split_axis=0, concat_axis=0, tiled=True
    )
    return jnp.sum(arrived, axis=0)


def shards(queries, indices, first_keys, second_keys, values):
    seqs_dev, head_count, top_count = indices.shape
    half_width = queries.shape[2] // 2
    table_rows, value_width = values.shape
    sub_count = second_keys.shape[1]
    devices = lax.axis_size(("table", "batch"))
    entries = seqs_dev * head_count * top_count
    slot_cap = max(2, 2 * entries // devices)
    positions = jnp.arange(entries, dtype=jnp.int32)
    entry_seq = positions // (head_count * top_count)
    entry_head = positions // top_count % head_count
    flat_index = indices.reshape(entries)
    row_owner = flat_index // table_rows
    local_row = flat_index % table_rows
    entry_codes = (entry_seq * head_count + entry_head) * table_rows + local_row
    owner_hot = (row_owner[:, None] == jnp.arange(devices, dtype=jnp.int32)[None, :]).astype(
        jnp.int32
    )
    slot_rank = jnp.sum(jnp.cumsum(owner_hot, axis=0) * owner_hot, axis=1) - 1
    slot_index = row_owner * slot_cap + slot_rank
    placed = slot_index[:, None] == jnp.arange(devices * slot_cap, dtype=jnp.int32)[None, :]
    query_entries = jnp.broadcast_to(
        queries[:, :, None, :], (seqs_dev, head_count, top_count, 2 * half_width)
    ).reshape(entries, 2 * half_width)
    query_slots = lax.dot_general(
        placed.astype(jnp.bfloat16),
        query_entries[:, :half_width],
        (((0,), (0,)), ((), ())),
        preferred_element_type=jnp.float32,
    )
    query_slots = query_slots.astype(jnp.bfloat16).reshape(devices, slot_cap, half_width)
    code_slots = (jnp.sum(jnp.where(placed, entry_codes[:, None] + 1, 0), axis=0) - 1).reshape(
        devices, slot_cap
    )
    first_slots, fetched, seq_local = answer_slots(
        (
            lax.all_to_all(
                query_slots, ("table", "batch"), split_axis=0, concat_axis=0, tiled=True
            ),
            lax.all_to_all(code_slots, ("table", "batch"), split_axis=0, concat_axis=0, tiled=True),
        ),
        first_keys,
        values,
    )
    returned = lax.all_to_all(
        first_slots, ("table", "batch"), split_axis=0, concat_axis=0, tiled=True
    ).reshape(devices * slot_cap)
    first_entries = jnp.sum(jnp.where(placed, returned[None, :], 0.0), axis=1)
    second_entries = second_scores(
        query_entries[:, half_width:], entry_head, flat_index % sub_count, second_keys
    )
    scores = (first_entries + second_entries).reshape(seqs_dev, head_count, top_count)
    best_score = jnp.max(scores, axis=-1, keepdims=True)
    raised = jnp.exp(scores - best_score)
    weights = (raised / jnp.sum(raised, axis=-1, keepdims=True)).astype(jnp.bfloat16)
    slot_weights = jnp.sum(
        jnp.where(placed, weights.reshape(entries).astype(jnp.float32)[:, None], 0.0), axis=0
    ).astype(jnp.bfloat16)
    arrived = lax.all_to_all(
        slot_weights.reshape(devices, slot_cap),
        ("table", "batch"),
        split_axis=0,
        concat_axis=0,
        tiled=True,
    )
    output = combine_home(arrived, fetched, seq_local, seqs_dev)
    return output.astype(jnp.bfloat16)


def solution(mesh):
    placed = (
        P(("table", "batch"), None, None),
        P(("table", "batch"), None, None),
        P(None, ("table", "batch"), None),
        P(),
        P(("table", "batch"), None),
    )
    return jax.shard_map(
        shards, mesh=mesh, in_specs=placed, out_specs=P(("table", "batch"), None), check_vma=False
    )
```

profile of v0, /device:TPU:0, one launch (start us, length us, event | category | flops | bytes accessed | tf_op | source)
XLA Modules:
  0.0 100.8 jit_solution(396019297459717824)
XLA Ops:
  0.0 0.0 copy-start
  0.0 0.0 copy-start.1
  0.0 0.9 reshape.419
  0.9 0.8 reshape.420
  1.8 1.2 %reduce-window.6 = s32[32,4,128]{2,0,1:T(8,128)S(1)} reduce-window(s32[32,4,128]{2,0,1:T(8,128)S(1)} %fusion.14, s32[]{:T(128)} %constant.143.clone.1), window={size=1x1x128 pad=0_0x0_0x127_0}, to_apply=%region_0.1 | reduce-window | flops 2080768 | bytes 131076 | tf_op jit(solution)/shard_map/reduce-window
  2.9 0.2 slice_reduce_fusion
  3.2 0.1 fusion.13
  3.3 0.3 select_reduce_fusion.2
  3.6 0.7 sub.67
  4.3 7.3 %all-to-all-start = ((s32[32,1,32]{2,1,0:T(1,128)}), s32[32,1,32]{2,1,0:T(1,128)S(1)}, u32[]{:S(2)}, u32[]{:S(2)}) async-start(s32[32,1,32]{2,1,0:T(1,128)} %sub.67), calls=%async_computation | async-start | bytes 32768 | tf_op jit(solution)/shard_map/all_to_all | solution.py:102
  11.6 0.8 broadcast_in_dim.88
  12.4 1.6 %fusion.7 = bf16[1024,256]{1,0:T(8,128)(2,1)} fusion(s32[512]{0:T(512)S(1)} %add_add_fusion, bf16[512,512]{1,0:T(8,128)(2,1)S(1)} %bitcast.35), kind=kOutput, calls=%fused_computation.14 | convolution fusion | flops 269221888 | bytes 788480 | tf_op jit(solution)/shard_map/dot_general | solution.py:87
  14.0 0.0 copy-start.2
  14.0 4.8 %all-to-all-done = s32[32,1,32]{2,1,0:T(1,128)S(1)} async-done(((s32[32,1,32]{2,1,0:T(1,128)}), s32[32,1,32]{2,1,0:T(1,128)S(1)}, u32[]{:S(2)}, u32[]{:S(2)}) %all-to-all-start) | async-done | bytes 4128 | tf_op jit(solution)/shard_map/all_to_all | solution.py:102
  18.8 2.6 %all-to-all-start.1 = ((bf16[32,32,256]{2,1,0:T(8,128)(2,1)}), bf16[32,32,256]{2,1,0:T(8,128)(2,1)S(1)}, u32[]{:S(2)}, u32[]{:S(2)}) async-start(bf16[32,32,256]{2,1,0:T(8,128)(2,1)} %bitcast.3), calls=%async_computation.1 | async-start | bytes 1048576 | tf_op jit(solution)/shard_map/all_to_all | solution.py:99
  21.5 0.0 copy-done.1
  21.5 0.1 reshape.426
  21.6 0.0 copy-done
  21.6 2.0 %gather_fusion = bf16[512,256]{1,0:T(8,128)(2,1)S(1)} fusion(bf16[4096,256]{1,0:T(8,128)(2,1)S(1)} %bitcast.34, s32[1024]{0:T(1024)S(1)} %pad_clamp_fusion), kind=kCustom, calls=%fused_computation | custom fusion | bytes 526336 | tf_op jit(solution)/shard_map/jit(_take)/gather | solution.py:45
  23.6 0.2 multiply_reduce_fusion
  23.9 11.8 %all-to-all-done.1 = bf16[32,32,256]{2,1,0:T(8,128)(2,1)S(1)} async-done(((bf16[32,32,256]{2,1,0:T(8,128)(2,1)}), bf16[32,32,256]{2,1,0:T(8,128)(2,1)S(1)}, u32[]{:S(2)}, u32[]{:S(2)}) %all-to-all-start.1) | async-done | bytes 524320 | tf_op jit(solution)/shard_map/all_to_all | solution.py:99
  35.7 0.0 copy-done.2
  35.7 1.0 %fusion.8 = f32[32,32]{1,0:T(8,128)} fusion(bf16[32,32,256]{2,1,0:T(8,128)(2,1)S(1)} %all-to-all-done.1, s32[32,32]{1,0:T(8,128)S(1)} %get-tuple-element.5, bf16[4,8,256]{2,1,0:T(8,128)(2,1)S(1)} %copy-done.2), kind=kOutput, calls=%fused_computation.15 | convolution fusion | flops 17595392 | bytes 548864 | tf_op jit(solution)/shard_map/dnc,ck->dnk/dot_general | solution.py:25
  36.7 4.1 %all-to-all-start.2 = ((f32[32,1,32]{2,1,0:T(1,128)}), f32[32,1,32]{2,1,0:T(1,128)S(1)}, u32[]{:S(2)}, u32[]{:S(2)}) async-start(f32[32,1,32]{2,1,0:T(1,128)} %bitcast.7), calls=%async_computation.2 | async-start | bytes 32768 | tf_op jit(solution)/shard_map/all_to_all | solution.py:107
  40.9 25.0 %fusion.1 = bf16[32,32,1024]{2,1,0:T(8,128)(2,1)} fusion(bf16[8192,1024]{1,0:T(8,128)(2,1)} %param.9, s32[32,32]{1,0:T(8,128)S(1)} %get-tuple-element.6), kind=kOutput, calls=%fused_computation.3 | convolution fusion | flops 17188257792 | bytes 18878464 | tf_op jit(solution)/shard_map/dnv,vc->dnc/dot_general | solution.py:35
  65.9 0.0 all-to-all-done.2
  65.9 0.5 broadcast.618
  66.4 0.7 reduce.5
  67.1 0.1 broadcast_in_dim.89
  67.2 0.4 select_reduce_fusion.1
  67.6 0.1 add.223
  67.7 0.1 reduce_max.9
  67.7 0.2 fusion
  67.9 0.1 div.112
  68.0 0.1 sub.72
  68.1 0.1 sub.73
  68.2 0.3 select_reduce_fusion
  68.5 0.7 convert_element_type.66
  69.2 5.8 %all-to-all-start.3 = ((bf16[32,1,32]{2,1,0:T(2,128)(2,1)}), bf16[32,1,32]{2,1,0:T(2,128)(2,1)S(1)}, u32[]{:S(2)}, u32[]{:S(2)}) async-start(bf16[32,1,32]{2,1,0:T(2,128)(2,1)} %convert_element_type.66), calls=%async_computation.3 | async-start | bytes 32768 | tf_op jit(solution)/shard_map/all_to_all | solution.py:121
  75.0 0.1 compare_select_fusion
  75.1 7.1 %all-to-all-done.3 = bf16[32,1,32]{2,1,0:T(2,128)(2,1)S(1)} async-done(((bf16[32,1,32]{2,1,0:T(2,128)(2,1)}), bf16[32,1,32]{2,1,0:T(2,128)(2,1)S(1)}, u32[]{:S(2)}, u32[]{:S(2)}) %all-to-all-start.3) | async-done | bytes 2080 | tf_op jit(solution)/shard_map/all_to_all | solution.py:121
  82.2 2.0 %fusion.4 = f32[32,4,1024]{2,1,0:T(4,128)S(1)} fusion(bf16[32,32,1024]{2,1,0:T(8,128)(2,1)} %fusion.1, s32[32,32]{1,0:T(8,128)S(1)} %bitcast.38, bf16[32,32]{1,0:T(8,128)(2,1)S(1)} %bitcast.39), kind=kOutput, calls=%fused_computation.6 | convolution fusion | flops 8396800 | bytes 2627584 | tf_op jit(solution)/shard_map/dsc,dcv->dsv/dot_general | solution.py:56
  84.2 16.0 %all_to_all.34 = f32[32,4,1024]{2,1,0:T(4,128)S(1)} all-to-all(f32[32,4,1024]{2,1,0:T(4,128)S(1)} %fusion.4), channel_id=1, replica_groups=mesh['table'=8,'batch'=4] {'table','batch'}, dimensions={0} | all-to-all | bytes 1048576 | tf_op jit(solution)/shard_map/all_to_all | solution.py:57
  100.2 0.7 reduce_sum.79
  (14 shorter events, 0.2 us)
Async XLA Ops:
  0.0 21.6 %copy-start = (bf16[4,1024,256]{2,1,0:T(8,128)(2,1)S(1)}, bf16[4,1024,256]{2,1,0:T(8,128)(2,1)}, u32[]{:S(2)}) copy-start(bf16[4,1024,256]{2,1,0:T(8,128)(2,1)} %param.8) | copy-start | bytes 6291460
  0.0 21.5 %copy-start.1 = (s32[4,4,32]{2,1,0:T(4,128)S(1)}, s32[4,4,32]{2,1,0:T(4,128)}, u32[]{:S(2)}) copy-start(s32[4,4,32]{2,1,0:T(4,128)} %param.6) | copy-start | bytes 6148
  4.3 14.5 %all-to-all-start = ((s32[32,1,32]{2,1,0:T(1,128)}), s32[32,1,32]{2,1,0:T(1,128)S(1)}, u32[]{:S(2)}, u32[]{:S(2)}) async-start(s32[32,1,32]{2,1,0:T(1,128)} %sub.67), calls=%async_computation | async-start | bytes 32768 | tf_op jit(solution)/shard_map/all_to_all | solution.py:102
  14.0 21.7 %copy-start.2 = (bf16[4,8,256]{2,1,0:T(8,128)(2,1)S(1)}, bf16[4,8,256]{2,1,0:T(8,128)(2,1)}, u32[]{:S(2)}) copy-start(bf16[4,8,256]{2,1,0:T(8,128)(2,1)} %param.7) | copy-start | bytes 49156
  18.8 16.9 %all-to-all-start.1 = ((bf16[32,32,256]{2,1,0:T(8,128)(2,1)}), bf16[32,32,256]{2,1,0:T(8,128)(2,1)S(1)}, u32[]{:S(2)}, u32[]{:S(2)}) async-start(bf16[32,32,256]{2,1,0:T(8,128)(2,1)} %bitcast.3), calls=%async_computation.1 | async-start | bytes 1048576 | tf_op jit(solution)/shard_map/all_to_all | solution.py:99
  36.7 29.2 %all-to-all-start.2 = ((f32[32,1,32]{2,1,0:T(1,128)}), f32[32,1,32]{2,1,0:T(1,128)S(1)}, u32[]{:S(2)}, u32[]{:S(2)}) async-start(f32[32,1,32]{2,1,0:T(1,128)} %bitcast.7), calls=%async_computation.2 | async-start | bytes 32768 | tf_op jit(solution)/shard_map/all_to_all | solution.py:107
  69.2 13.0 %all-to-all-start.3 = ((bf16[32,1,32]{2,1,0:T(2,128)(2,1)}), bf16[32,1,32]{2,1,0:T(2,128)(2,1)S(1)}, u32[]{:S(2)}, u32[]{:S(2)}) async-start(bf16[32,1,32]{2,1,0:T(2,128)(2,1)} %convert_element_type.66), calls=%async_computation.3 | async-start | bytes 32768 | tf_op jit(solution)/shard_map/all_to_all | solution.py:121
where the time goes:
time: 102 us; the launch traced here: 101 us
  matrix products  29.7 us (29%)
  waiting for transfers between devices  23.8 us (23%)
  starting transfers between devices  19.9 us (20%)
  blocking collectives  16 us (16%)
  local copies, waits for them, and re-layouts  7.03 us (7%)
  other arithmetic  4.36 us (4%)
    dot_general x1, matrix products, answer_slots(): jnp.einsum('dnv,vc->dnc', row_pick, values, preferred_element_type=jnp.fl...  25 us
    all_to_all x1, blocking collectives, combine_home(): lax.all_to_all(owner_part, ('table', 'batch'), split_axis=0, concat_axis=...  16 us
    all_to_all x1, waiting for transfers between devices, shards(): lax.all_to_all(query_slots, ('table', 'batch'), split_axis=0, concat_axis...  11.8 us
    all_to_all x1, starting transfers between devices, shards(): lax.all_to_all(code_slots, ('table', 'batch'), split_axis=0, concat_axis=...  7.33 us
    all_to_all x1, waiting for transfers between devices, shards(): lax.all_to_all(slot_weights.reshape(devices, slot_cap), ('table', 'batch'...  7.11 us
    all_to_all x1, starting transfers between devices, shards(): lax.all_to_all(slot_weights.reshape(devices, slot_cap), ('table', 'batch'...  5.83 us
    all_to_all x1, waiting for transfers between devices, shards(): lax.all_to_all(code_slots, ('table', 'batch'), split_axis=0, concat_axis=...  4.82 us
    all_to_all x1, starting transfers between devices, shards(): lax.all_to_all(first_slots, ('table', 'batch'), split_axis=0, concat_axis...  4.14 us
  transfers between devices with their start and end apart: 4, of which 3 were waited for; matrix products, arithmetic and copies ran while one was open for 30% of the time, Pallas kernels for 0%

commit v1 on v0

v1 whole, which is shorter than its diff:
```python
import functools

import jax
import jax.numpy as jnp
from jax import lax
from jax.experimental import pallas as pl
from jax.experimental.pallas import tpu as pltpu
from jax.sharding import PartitionSpec as P

MESH = pl.DeviceIdType.MESH
LANES = 128
NT = (((1,), (1,)), ((), ()))


def log2(number):
    assert number & (number - 1) == 0
    return number.bit_length() - 1


def pick_lanes(table, ids):
    picked = jnp.zeros(ids.shape, jnp.float32)
    inner = ids & (LANES - 1)
    outer = lax.shift_right_arithmetic(ids, 7)
    for part in range(table.shape[1] // LANES):
        got = jnp.take_along_axis(table[:, part * LANES : (part + 1) * LANES], inner, axis=1)
        picked = jnp.where(outer == part, got, picked)
    return picked


def kernel(
    shape,
    q_ref,
    i_ref,
    fk_ref,
    sk_ref,
    v_ref,
    out_ref,
    vbuf,
    k2buf,
    kslot,
    islot,
    icomp,
    qslot,
    qrows,
    grows,
    rolled,
    wpack,
    wslot,
    istage,
    wstage,
    wfin,
    wacc,
    wb,
    psend,
    pslot,
    v_sem,
    k2_sem,
    k_send,
    k_recv,
    i_send,
    i_recv,
    q_send,
    q_recv,
    w_send,
    w_recv,
    p_send,
    p_recv,
):
    nt, nb, heads, seqs, top, chunks, pieces = shape
    devices = nt * nb
    groups = devices // heads
    half = q_ref.shape[2] // 2
    rows, width = v_ref.shape
    t_me, b_me = lax.axis_index("table"), lax.axis_index("batch")
    dev_me = t_me * nb + b_me
    head_me = lax.rem(t_me, heads)
    group_me = lax.div(t_me, heads) * nb + b_me
    slot_me = head_me * groups + group_me

    def place(slot):
        head = lax.div(slot, groups)
        group = lax.rem(slot, groups)
        return lax.div(group, nb) * heads + head, lax.rem(group, nb), head

    def others(body):
        def step(offset, carry):
            slot = lax.rem(slot_me + offset, devices)
            t, b, head = place(slot)
            body(slot, (t, b), head)
            return carry

        lax.fori_loop(1, devices, step, 0)

    def drain(ref, sem):
        pltpu.make_async_copy(ref, ref, sem).wait()

    k2_copy = pltpu.make_async_copy(sk_ref.at[head_me], k2buf, k2_sem)
    k2_copy.start()
    block = rows // pieces
    v_copies = [
        pltpu.make_async_copy(
            v_ref.at[pl.ds(p * block, block)], vbuf.at[pl.ds(p * block, block)], v_sem.at[p]
        )
        for p in range(pieces)
    ]
    for copy in v_copies:
        copy.start()

    barrier = pltpu.get_barrier_semaphore()
    others(
        lambda slot, where, head: pl.semaphore_signal(
            barrier, inc=1, device_id=where, device_id_type=MESH
        )
    )
    for h in range(heads):
        for s in range(seqs):
            icomp[pl.ds(s, 1), pl.ds(h * top, top)] = i_ref[s, pl.ds(h, 1), :]
    islot[slot_me] = icomp[...]
    kslot[dev_me] = fk_ref[head_me]
    qslot[head_me] = q_ref[...]
    pl.semaphore_wait(barrier, devices - 1)

    def send_q(j):
        other = lax.rem(head_me + j, heads)
        pltpu.make_async_remote_copy(
            src_ref=q_ref,
            dst_ref=qslot.at[head_me],
            send_sem=q_send,
            recv_sem=q_recv,
            device_id=(lax.div(t_me, heads) * heads + other, b_me),
            device_id_type=MESH,
        ).start()

    for j in range(1, heads):
        send_q(j)

    def send_keys(slot, where, head):
        pltpu.make_async_remote_copy(
            src_ref=fk_ref.at[head],
            dst_ref=kslot.at[dev_me],
            send_sem=k_send,
            recv_sem=k_recv,
            device_id=where,
            device_id_type=MESH,
        ).start()

    def send_ids(slot, where, head):
        pltpu.make_async_remote_copy(
            src_ref=icomp,
            dst_ref=islot.at[slot_me],
            send_sem=i_send,
            recv_sem=i_recv,
            device_id=where,
            device_id_type=MESH,
        ).start()

    others(send_keys)
    others(send_ids)

    drain(qslot.at[pl.ds(0, heads - 1)], q_recv)
    for j in range(heads):
        for s in range(seqs):
            one = qslot[j, s].astype(jnp.float32)
            for c in range(qrows.shape[0]):
                qrows[c, pl.ds((j * seqs + s) * heads, heads), :] = one[
                    :, c * LANES : (c + 1) * LANES
                ]
    q_all = jnp.concatenate(
        [
            qrows.at[c][pl.ds(head_me, heads * seqs, stride=heads), :]
            for c in range(qrows.shape[0])
        ],
        axis=1,
    ).astype(jnp.bfloat16)
    k2_copy.wait()
    s2 = lax.dot_general(q_all[:, half:], k2buf[...], NT, preferred_element_type=jnp.float32)
    drain(islot.at[pl.ds(0, devices - 1)], i_recv)
    for j in range(heads):
        grows[pl.ds(j * seqs, seqs), :] = islot[j * groups + group_me]
    ids = grows[...]
    sub_count = k2buf.shape[0]
    second = pick_lanes(s2, ids & (sub_count - 1))
    for slot in range(devices):
        istage[pl.ds(slot * seqs, seqs), :] = islot[slot]
    drain(kslot.at[pl.ds(0, devices - 1)], k_recv)
    k1 = kslot[...].astype(jnp.float32)
    k1 = k1.reshape(k1.shape[0] * k1.shape[1], half).astype(jnp.bfloat16)
    s1 = lax.dot_general(q_all[:, :half], k1, NT, preferred_element_type=jnp.float32)
    score = second + pick_lanes(s1, lax.shift_right_arithmetic(ids, log2(sub_count)))
    lane = lax.broadcasted_iota(jnp.int32, ids.shape, 1)
    mine = lax.shift_right_arithmetic(lane, log2(top)) == head_me
    best = jnp.max(jnp.where(mine, score, -jnp.inf), axis=1, keepdims=True)
    raised = jnp.where(mine, jnp.exp(jnp.where(mine, score - best, 0.0)), 0.0)
    weights = raised / jnp.sum(raised, axis=1, keepdims=True)
    weights = weights.astype(jnp.bfloat16).astype(jnp.float32)
    for j in range(heads):
        rolled[j] = pltpu.roll(weights, lax.rem(j - head_me + heads, heads) * top, 1)
    packed = rolled[0, pl.ds(0, seqs), :]
    for j in range(1, heads):
        packed = packed + rolled[j, pl.ds(j * seqs, seqs), :]
    wpack[...] = packed
    wslot[slot_me] = packed

    def send_weights(slot, where, head):
        pltpu.make_async_remote_copy(
            src_ref=wpack,
            dst_ref=wslot.at[slot_me],
            send_sem=w_send,
            recv_sem=w_recv,
            device_id=where,
            device_id_type=MESH,
        ).start()

    others(send_weights)
    drain(wslot.at[pl.ds(0, devices - 1)], w_recv)
    for slot in range(devices):
        wstage[pl.ds(slot * seqs, seqs), :] = wslot[slot]
    span = groups * seqs
    lane = lax.broadcasted_iota(jnp.int32, (span, LANES), 1)
    block_of = lax.shift_right_arithmetic(lane, log2(top))
    for j in range(heads):
        total = jnp.zeros((span, LANES), jnp.float32)
        for h in range(heads):
            part = wstage[pl.ds(h * span, span), :]
            if h != j:
                part = pltpu.roll(part, (h - j) % heads * top, 1)
            total = jnp.where(block_of == h, part, total)
        wfin[pl.ds(j * span, span), :] = total

    high_count = rows // LANES
    all_seqs = devices * seqs
    high_iota = lax.broadcasted_iota(jnp.int32, (high_count, LANES), 0)
    low_iota = lax.broadcasted_iota(jnp.int32, (LANES, LANES), 0)
    base = dev_me * rows

    def spread(step, carry):
        for u in range(8):
            s = step * 8 + u
            row = istage[pl.ds(s, 1), :]
            high = lax.shift_right_arithmetic(row - base, 7)
            low = row & (LANES - 1)
            left = jnp.where(high_iota == high, wfin[pl.ds(s, 1), :], 0.0).astype(jnp.bfloat16)
            right = jnp.where(low_iota == low, 1.0, 0.0).astype(jnp.bfloat16)
            wacc[pl.ds(s, high_count, stride=all_seqs), :] = lax.dot_general(
                left, right, NT, preferred_element_type=jnp.float32
            )
        return carry

    lax.fori_loop(0, all_seqs // 8, spread, 0)

    def narrow(step, carry):
        wb[:, pl.ds(pl.multiple_of(step * LANES, LANES), LANES)] = wacc[
            pl.ds(pl.multiple_of(step * all_seqs, all_seqs), all_seqs), :
        ].astype(jnp.bfloat16)
        return carry

    lax.fori_loop(0, high_count, narrow, 0)
    for copy in v_copies:
        copy.wait()

    piece = width // chunks
    deep = min(1024, rows)
    for c in range(chunks):

        def multiply(step, acc):
            at = pl.multiple_of(step * deep, deep)
            return acc + jnp.dot(
                wb[:, pl.ds(at, deep)],
                vbuf[pl.ds(at, deep), pl.ds(c * piece, piece)],
                preferred_element_type=jnp.float32,
            )

        acc = lax.fori_loop(
            0, rows // deep, multiply, jnp.zeros((all_seqs, piece), jnp.float32)
        )
        for slot in range(devices):
            psend[c, slot] = acc[slot * seqs : (slot + 1) * seqs, :].astype(jnp.bfloat16)
        pslot[c, slot_me] = psend[c, slot_me]

        def send_part(slot, where, head):
            pltpu.make_async_remote_copy(
                src_ref=psend.at[c, slot],
                dst_ref=pslot.at[c, slot_me],
                send_sem=p_send.at[c],
                recv_sem=p_recv.at[c],
                device_id=where,
                device_id_type=MESH,
            ).start()

        others(send_part)

    for c in range(chunks):
        drain(pslot.at[c, pl.ds(0, devices - 1)], p_recv.at[c])
        total = jnp.zeros((seqs, piece), jnp.float32)
        for slot in range(devices):
            total = total + pslot[c, slot].astype(jnp.float32)
        out_ref[:, pl.ds(c * piece, piece)] = total.astype(jnp.bfloat16)

    drain(qslot.at[pl.ds(0, heads - 1)], q_send)
    drain(kslot.at[pl.ds(0, devices - 1)], k_send)
    drain(islot.at[pl.ds(0, devices - 1)], i_send)
    drain(wslot.at[pl.ds(0, devices - 1)], w_send)
    for c in range(chunks):
        drain(pslot.at[c, pl.ds(0, devices - 1)], p_send.at[c])


def shards(nt, nb, queries, indices, first_keys, second_keys, values):
    seqs, heads, top = indices.shape
    width_q = queries.shape[2]
    half = width_q // 2
    firsts = first_keys.shape[1]
    sub_count = second_keys.shape[1]
    rows, width = values.shape
    devices = nt * nb
    all_seqs = devices * seqs
    assert heads * top == LANES and nt % heads == 0
    chunks, pieces = 4, 4
    vmem = pl.BlockSpec(memory_space=pltpu.VMEM)
    hbm = pl.BlockSpec(memory_space=pl.ANY)
    dma = pltpu.SemaphoreType.DMA
    return pl.pallas_call(
        functools.partial(kernel, (nt, nb, heads, seqs, top, chunks, pieces)),
        out_shape=jax.ShapeDtypeStruct((seqs, width), jnp.bfloat16),
        in_specs=[vmem, vmem, vmem, hbm, hbm],
        out_specs=vmem,
        scratch_shapes=[
            pltpu.VMEM((rows, width), jnp.bfloat16),
            pltpu.VMEM((sub_count, half), jnp.bfloat16),
            pltpu.VMEM((devices, firsts, half), jnp.bfloat16),
            pltpu.VMEM((devices, seqs, LANES), jnp.int32),
            pltpu.VMEM((seqs, LANES), jnp.int32),
            pltpu.VMEM((heads, seqs, heads, width_q), jnp.bfloat16),
            pltpu.VMEM((width_q // LANES, heads * seqs * heads, LANES), jnp.float32),
            pltpu.VMEM((heads * seqs, LANES), jnp.int32),
            pltpu.VMEM((heads, heads * seqs, LANES), jnp.float32),
            pltpu.VMEM((seqs, LANES), jnp.float32),
            pltpu.VMEM((devices, seqs, LANES), jnp.float32),
            pltpu.VMEM((all_seqs, LANES), jnp.int32),
            pltpu.VMEM((all_seqs, LANES), jnp.float32),
            pltpu.VMEM((all_seqs, LANES), jnp.float32),
            pltpu.VMEM((rows // LANES * all_seqs, LANES), jnp.float32),
            pltpu.VMEM((all_seqs, rows), jnp.bfloat16),
            pltpu.VMEM((chunks, devices, seqs, width // chunks), jnp.bfloat16),
            pltpu.VMEM((chunks, devices, seqs, width // chunks), jnp.bfloat16),
            dma((pieces,)),
            dma,
            dma,
            dma,
            dma,
            dma,
            dma,
            dma,
            dma,
            dma,
            dma((chunks,)),
            dma((chunks,)),
        ],
        compiler_params=pltpu.CompilerParams(
            collective_id=0, has_side_effects=True, vmem_limit_bytes=60 * 1024 * 1024
        ),
    )(queries, indices, first_keys, second_keys, values)


def solution(mesh):
    placed = (
        P(("table", "batch"), None, None),
        P(("table", "batch"), None, None),
        P(None, ("table", "batch"), None),
        P(),
        P(("table", "batch"), None),
    )
    body = functools.partial(shards, mesh.shape["table"], mesh.shape["batch"])
    return jax.shard_map(
        body, mesh=mesh, in_specs=placed, out_specs=P(("table", "batch"), None), check_vma=False
    )
```

time: 102 us -> 42.5 us (0.42)
  Pallas kernels: 0 us -> 40.8 us
  matrix products: 29.7 us -> 0 us
  waiting for transfers between devices: 23.8 us -> 0 us
  starting transfers between devices: 19.9 us -> 0 us
  blocking collectives: 16 us -> 0 us
  local copies, waits for them, and re-layouts: 7.03 us -> 1.3 us
  other arithmetic: 4.36 us -> 0 us
    pallas_call x0 -> x1, Pallas kernels: none -> 40.8 us  [shards(): pl.pallas_call(functools.partial(kernel, (nt, nb, heads, seqs, top, chunk...]
    dot_general x4 -> x0, matrix products: 29.7 us -> none  [the longest x1 25 us: answer_slots(): jnp.einsum('dnv,vc->dnc', row_pick, values, preferred_element_type=jnp.fl...]
    all_to_all x4 -> x0, waiting for transfers between devices: 23.8 us -> none  [the longest x1 11.8 us: shards(): lax.all_to_all(query_slots, ('table', 'batch'), split_axis=0, concat_axis...]
    all_to_all x4 -> x0, starting transfers between devices: 19.9 us -> none  [the longest x1 7.33 us: shards(): lax.all_to_all(code_slots, ('table', 'batch'), split_axis=0, concat_axis=...]
    all_to_all x1 -> x0, blocking collectives: 16 us -> none  [combine_home(): lax.all_to_all(owner_part, ('table', 'batch'), split_axis=0, concat_axis=...]
    reduce_sum x6 -> x0, other arithmetic: 1.99 us -> none  [the longest x1 0.7 us: combine_home(): return jnp.sum(arrived, axis=0)]
    gather x1 -> x0, local copies, waits for them, and re-layouts: 1.95 us -> none  [second_scores(): key_rows = jnp.take(key_table, where_rows, axis=0)]
    reshape x3 -> x0, local copies, waits for them, and re-layouts: 1.81 us -> none  [shards(): flat_index = indices.reshape(entries)]
  transfers between devices with their start and end apart: 4 -> 0, of which waited for: 3 -> 0; matrix products, arithmetic and copies ran while one was open for 30% -> 0% of each run, Pallas kernels for 0% -> 0%
where the time goes in v1:
time: 42.5 us; the launch traced here: 42.1 us
  Pallas kernels  40.8 us (96%)
  local copies, waits for them, and re-layouts  1.3 us (3%)
    pallas_call x1, Pallas kernels, shards(): pl.pallas_call(functools.partial(kernel, (nt, nb, heads, seqs, top, chunk...  40.8 us
    unnamed x1, local copies, waits for them, and re-layouts  1.3 us

profile of v1, /device:TPU:0, one launch (start us, length us, event | category | flops | bytes accessed | tf_op | source)
XLA Modules:
  0.0 42.1 jit_solution(5936378864993017216)
XLA Ops:
  0.0 40.8 %shard_map.55 = bf16[4,1024]{1,0:T(4,128)(2,1)} custom-call(bf16[4,4,512]{2,1,0:T(4,128)(2,1)} %q_ref.1, s32[4,4,32]{2,1,0:T(4,128)} %i_ref.1, bf16[4,8,256]{2,1,0:T(8,128)(2,1)} %fk_ref.1, bf16[4,1024,256]{2,1,0:T(8,128)(2,1)} %sk_ref.1, bf16[8192,1024]{1,0:T(8,128)(2,1)} %v_ref.1), custom_call_target="tpu_custom_call" | custom-call | tf_op jit(solution)/shard_map/pallas_call | solution.py:321
  40.8 1.3 %copy.7 = bf16[4,1024]{1,0:T(4,128)(2,1)} copy(bf16[4,1024]{1,0:T(4,128)(2,1)} %shard_map.55) | data formatting | bytes 16384

commit v2 on v1

--- a/solution.py
+++ b/solution.py
@@ -10,6 +10,7 @@
 MESH = pl.DeviceIdType.MESH
 LANES = 128
 NT = (((1,), (1,)), ((), ()))
+NN = (((1,), (0,)), ((), ()))
 
 
 def log2(number):
@@ -39,6 +40,7 @@
     k2buf,
     kslot,
     islot,
+    gslot,
     icomp,
     qslot,
     qrows,
@@ -51,6 +53,9 @@
     wfin,
     wacc,
     wb,
+    lows,
+    accs,
+    pair,
     psend,
     pslot,
     v_sem,
@@ -59,14 +64,18 @@
     k_recv,
     i_send,
     i_recv,
+    g_send,
+    g_recv,
     q_send,
     q_recv,
     w_send,
     w_recv,
+    a_send,
+    a_recv,
     p_send,
     p_recv,
 ):
-    nt, nb, heads, seqs, top, chunks, pieces = shape
+    nt, nb, heads, seqs, top, chunks, pieces, early = shape
     devices = nt * nb
     groups = devices // heads
     half = q_ref.shape[2] // 2
@@ -77,19 +86,21 @@
     group_me = lax.div(t_me, heads) * nb + b_me
     slot_me = head_me * groups + group_me
 
-    def place(slot):
-        head = lax.div(slot, groups)
-        group = lax.rem(slot, groups)
-        return lax.div(group, nb) * heads + head, lax.rem(group, nb), head
-
-    def others(body):
-        def step(offset, carry):
-            slot = lax.rem(slot_me + offset, devices)
-            t, b, head = place(slot)
-            body(slot, (t, b), head)
+    def others(body, stride=1):
+        def visit(shift, first):
+            t = lax.rem(t_me + shift * stride, nt)
+            head = lax.rem(t, heads)
+            start = head * groups + lax.div(t, heads) * nb
+            for k in range(first, nb):
+                b = lax.rem(b_me + k, nb)
+                body(start + b, (t, b), head)
+
+        def step(shift, carry):
+            visit(shift, 0)
             return carry
 
-        lax.fori_loop(1, devices, step, 0)
+        visit(0, 1)
+        lax.fori_loop(1, nt // stride, step, 0)
 
     def drain(ref, sem):
         pltpu.make_async_copy(ref, ref, sem).wait()
@@ -117,6 +128,7 @@
             icomp[pl.ds(s, 1), pl.ds(h * top, top)] = i_ref[s, pl.ds(h, 1), :]
     islot[slot_me] = icomp[...]
     kslot[dev_me] = fk_ref[head_me]
+    gslot[head_me] = icomp[...]
     qslot[head_me] = q_ref[...]
     pl.semaphore_wait(barrier, devices - 1)
 
@@ -131,8 +143,20 @@
             device_id_type=MESH,
         ).start()
 
+    def send_group_ids(j):
+        other = lax.rem(head_me + j, heads)
+        pltpu.make_async_remote_copy(
+            src_ref=icomp,
+            dst_ref=gslot.at[head_me],
+            send_sem=g_send,
+            recv_sem=g_recv,
+            device_id=(lax.div(t_me, heads) * heads + other, b_me),
+            device_id_type=MESH,
+        ).start()
+
     for j in range(1, heads):
         send_q(j)
+        send_group_ids(j)
 
     def send_keys(slot, where, head):
         pltpu.make_async_remote_copy(
@@ -174,14 +198,12 @@
     ).astype(jnp.bfloat16)
     k2_copy.wait()
     s2 = lax.dot_general(q_all[:, half:], k2buf[...], NT, preferred_element_type=jnp.float32)
-    drain(islot.at[pl.ds(0, devices - 1)], i_recv)
+    drain(gslot.at[pl.ds(0, heads - 1)], g_recv)
     for j in range(heads):
-        grows[pl.ds(j * seqs, seqs), :] = islot[j * groups + group_me]
+        grows[pl.ds(j * seqs, seqs), :] = gslot[j]
     ids = grows[...]
     sub_count = k2buf.shape[0]
     second = pick_lanes(s2, ids & (sub_count - 1))
-    for slot in range(devices):
-        istage[pl.ds(slot * seqs, seqs), :] = islot[slot]
     drain(kslot.at[pl.ds(0, devices - 1)], k_recv)
     k1 = kslot[...].astype(jnp.float32)
     k1 = k1.reshape(k1.shape[0] * k1.shape[1], half).astype(jnp.bfloat16)
@@ -212,6 +234,35 @@
         ).start()
 
     others(send_weights)
+    high_count = rows // LANES
+    all_seqs = devices * seqs
+    high_iota = lax.broadcasted_iota(jnp.int32, (high_count, LANES), 0)
+    low_iota = lax.broadcasted_iota(jnp.int32, (LANES, LANES), 0)
+    base = dev_me * rows
+
+    def high_hot(s, value):
+        high = lax.shift_right_arithmetic(istage[pl.ds(s, 1), :] - base, 7)
+        return jnp.where(high_iota == high, value, 0.0).astype(jnp.bfloat16)
+
+    def low_hot(s):
+        low = istage[pl.ds(s, 1), :] & (LANES - 1)
+        return jnp.where(low_iota == low, 1.0, 0.0).astype(jnp.bfloat16)
+
+    drain(islot.at[pl.ds(0, devices - 1)], i_recv)
+    for slot in range(devices):
+        istage[pl.ds(slot * seqs, seqs), :] = islot[slot]
+    low_lane = lax.broadcasted_iota(jnp.int32, (LANES, LANES), 1).astype(jnp.float32)
+    if early:
+
+        def build(step, carry):
+            some = istage[pl.ds(pl.multiple_of(step * 8, 8), 8), :] & (LANES - 1)
+            some = some.astype(jnp.float32).T
+            for u in range(8):
+                hot = jnp.where(low_lane == some[:, u : u + 1], 1.0, 0.0)
+                lows[step * 8 + u] = hot.astype(jnp.bfloat16)
+            return carry
+
+        lax.fori_loop(0, all_seqs // 8, build, 0)
     drain(wslot.at[pl.ds(0, devices - 1)], w_recv)
     for slot in range(devices):
         wstage[pl.ds(slot * seqs, seqs), :] = wslot[slot]
@@ -227,81 +278,88 @@
             total = jnp.where(block_of == h, part, total)
         wfin[pl.ds(j * span, span), :] = total
 
-    high_count = rows // LANES
-    all_seqs = devices * seqs
-    high_iota = lax.broadcasted_iota(jnp.int32, (high_count, LANES), 0)
-    low_iota = lax.broadcasted_iota(jnp.int32, (LANES, LANES), 0)
-    base = dev_me * rows
+    pitch = all_seqs + 8
 
     def spread(step, carry):
-        for u in range(8):
-            s = step * 8 + u
-            row = istage[pl.ds(s, 1), :]
-            high = lax.shift_right_arithmetic(row - base, 7)
-            low = row & (LANES - 1)
-            left = jnp.where(high_iota == high, wfin[pl.ds(s, 1), :], 0.0).astype(jnp.bfloat16)
-            right = jnp.where(low_iota == low, 1.0, 0.0).astype(jnp.bfloat16)
-            wacc[pl.ds(s, high_count, stride=all_seqs), :] = lax.dot_general(
-                left, right, NT, preferred_element_type=jnp.float32
+        for u in range(32):
+            s = step * 32 + u
+            left = high_hot(s, wfin[pl.ds(s, 1), :])
+            right = lows[s] if early else low_hot(s)
+            wacc[pl.ds(s, high_count, stride=pitch), :] = lax.dot_general(
+                left, right, NN if early else NT, preferred_element_type=jnp.float32
             )
         return carry
 
-    lax.fori_loop(0, all_seqs // 8, spread, 0)
+    lax.fori_loop(0, all_seqs // 32, spread, 0)
 
     def narrow(step, carry):
         wb[:, pl.ds(pl.multiple_of(step * LANES, LANES), LANES)] = wacc[
-            pl.ds(pl.multiple_of(step * all_seqs, all_seqs), all_seqs), :
+            pl.ds(pl.multiple_of(step * pitch, 8), all_seqs), :
         ].astype(jnp.bfloat16)
         return carry
 
-    lax.fori_loop(0, high_count, narrow, 0)
+    lax.fori_loop(0, high_count, narrow, 0, unroll=8)
     for copy in v_copies:
         copy.wait()
 
     piece = width // chunks
-    deep = min(1024, rows)
-    for c in range(chunks):
-
-        def multiply(step, acc):
-            at = pl.multiple_of(step * deep, deep)
-            return acc + jnp.dot(
-                wb[:, pl.ds(at, deep)],
-                vbuf[pl.ds(at, deep), pl.ds(c * piece, piece)],
-                preferred_element_type=jnp.float32,
-            )
-
-        acc = lax.fori_loop(
-            0, rows // deep, multiply, jnp.zeros((all_seqs, piece), jnp.float32)
-        )
-        for slot in range(devices):
-            psend[c, slot] = acc[slot * seqs : (slot + 1) * seqs, :].astype(jnp.bfloat16)
-        pslot[c, slot_me] = psend[c, slot_me]
+    core_me = lax.rem(t_me, 2)
+    half_slot = lax.div(head_me, 2) * groups + group_me
+
+    def pass_on(c):
+        drain(pair.at[c], a_recv.at[c])
+        for i in range(heads // 2):
+            both = accs[c, 2 * i + core_me] + pair[c, i]
+            for g in range(groups):
+                psend[c, i * groups + g] = both[g * seqs : (g + 1) * seqs, :].astype(jnp.bfloat16)
+        pslot[c, half_slot] = psend[c, half_slot]
 
         def send_part(slot, where, head):
             pltpu.make_async_remote_copy(
-                src_ref=psend.at[c, slot],
-                dst_ref=pslot.at[c, slot_me],
+                src_ref=psend.at[c, slot - lax.div(head + 1, 2) * groups],
+                dst_ref=pslot.at[c, half_slot],
                 send_sem=p_send.at[c],
                 recv_sem=p_recv.at[c],
                 device_id=where,
                 device_id_type=MESH,
             ).start()
 
-        others(send_part)
+        others(send_part, 2)
 
     for c in range(chunks):
-        drain(pslot.at[c, pl.ds(0, devices - 1)], p_recv.at[c])
+        acc = jnp.dot(
+            wb[...], vbuf[:, pl.ds(c * piece, piece)], preferred_element_type=jnp.float32
+        )
+        for j in range(heads):
+            accs[c, j] = acc[j * span : (j + 1) * span, :]
+        for i in range(heads // 2):
+            pltpu.make_async_remote_copy(
+                src_ref=accs.at[c, 2 * i + 1 - core_me],
+                dst_ref=pair.at[c, i],
+                send_sem=a_send.at[c],
+                recv_sem=a_recv.at[c],
+                device_id=(t_me + 1 - 2 * core_me, b_me),
+                device_id_type=MESH,
+            ).start()
+        if c > 0:
+            pass_on(c - 1)
+    pass_on(chunks - 1)
+
+    for c in range(chunks):
+        drain(pslot.at[c, pl.ds(0, devices // 2 - 1)], p_recv.at[c])
         total = jnp.zeros((seqs, piece), jnp.float32)
-        for slot in range(devices):
+        for slot in range(devices // 2):
             total = total + pslot[c, slot].astype(jnp.float32)
         out_ref[:, pl.ds(c * piece, piece)] = total.astype(jnp.bfloat16)
 
     drain(qslot.at[pl.ds(0, heads - 1)], q_send)
+    drain(gslot.at[pl.ds(0, heads - 1)], g_send)
     drain(kslot.at[pl.ds(0, devices - 1)], k_send)
     drain(islot.at[pl.ds(0, devices - 1)], i_send)
     drain(wslot.at[pl.ds(0, devices - 1)], w_send)
     for c in range(chunks):
-        drain(pslot.at[c, pl.ds(0, devices - 1)], p_send.at[c])
+        drain(pslot.at[c, pl.ds(0, devices // 2 - 1)], p_send.at[c])
+        drain(pair.at[c], a_send.at[c])
 
 
 def shards(nt, nb, queries, indices, first_keys, second_keys, values):
@@ -313,13 +371,14 @@
     rows, width = values.shape
     devices = nt * nb
     all_seqs = devices * seqs
-    assert heads * top == LANES and nt % heads == 0
-    chunks, pieces = 4, 4
+    assert heads * top == LANES and nt % heads == 0 and heads % 2 == 0
+    chunks, pieces = 2, 4
+    early = all_seqs <= 256
     vmem = pl.BlockSpec(memory_space=pltpu.VMEM)
     hbm = pl.BlockSpec(memory_space=pl.ANY)
     dma = pltpu.SemaphoreType.DMA
     return pl.pallas_call(
-        functools.partial(kernel, (nt, nb, heads, seqs, top, chunks, pieces)),
+        functools.partial(kernel, (nt, nb, heads, seqs, top, chunks, pieces, early)),
         out_shape=jax.ShapeDtypeStruct((seqs, width), jnp.bfloat16),
         in_specs=[vmem, vmem, vmem, hbm, hbm],
         out_specs=vmem,
@@ -328,6 +387,7 @@
             pltpu.VMEM((sub_count, half), jnp.bfloat16),
             pltpu.VMEM((devices, firsts, half), jnp.bfloat16),
             pltpu.VMEM((devices, seqs, LANES), jnp.int32),
+            pltpu.VMEM((heads, seqs, LANES), jnp.int32),
             pltpu.VMEM((seqs, LANES), jnp.int32),
             pltpu.VMEM((heads, seqs, heads, width_q), jnp.bfloat16),
             pltpu.VMEM((width_q // LANES, heads * seqs * heads, LANES), jnp.float32),
@@ -338,10 +398,13 @@
             pltpu.VMEM((all_seqs, LANES), jnp.int32),
             pltpu.VMEM((all_seqs, LANES), jnp.float32),
             pltpu.VMEM((all_seqs, LANES), jnp.float32),
-            pltpu.VMEM((rows // LANES * all_seqs, LANES), jnp.float32),
+            pltpu.VMEM((rows // LANES * (all_seqs + 8), LANES), jnp.float32),
             pltpu.VMEM((all_seqs, rows), jnp.bfloat16),
-            pltpu.VMEM((chunks, devices, seqs, width // chunks), jnp.bfloat16),
-            pltpu.VMEM((chunks, devices, seqs, width // chunks), jnp.bfloat16),
+            pltpu.VMEM((all_seqs if early else 1, LANES, LANES), jnp.bfloat16),
+            pltpu.VMEM((chunks, heads, all_seqs // heads, width // chunks), jnp.float32),
+            pltpu.VMEM((chunks, heads // 2, all_seqs // heads, width // chunks), jnp.float32),
+            pltpu.VMEM((chunks, devices // 2, seqs, width // chunks), jnp.bfloat16),
+            pltpu.VMEM((chunks, devices // 2, seqs, width // chunks), jnp.bfloat16),
             dma((pieces,)),
             dma,
             dma,
@@ -352,6 +415,10 @@
             dma,
             dma,
             dma,
+            dma,
+            dma,
+            dma((chunks,)),
+            dma((chunks,)),
             dma((chunks,)),
             dma((chunks,)),
         ],

time: 42.5 us -> 32.9 us (0.77)
  Pallas kernels: 40.8 us -> 31.3 us
    pallas_call x1, Pallas kernels: 40.8 us -> 31.3 us  [shards(): pl.pallas_call(functools.partial(kernel, (nt, nb, heads, seqs, top, chunk...]
where the time goes in v2:
time: 32.9 us; the launch traced here: 32.6 us
  Pallas kernels  31.3 us (95%)
  local copies, waits for them, and re-layouts  1.3 us (4%)
    pallas_call x1, Pallas kernels, shards(): pl.pallas_call(functools.partial(kernel, (nt, nb, heads, seqs, top, chunk...  31.3 us
    unnamed x1, local copies, waits for them, and re-layouts  1.3 us

profile of v2, /device:TPU:0, one launch (start us, length us, event | category | flops | bytes accessed | tf_op | source)
XLA Modules:
  0.0 32.6 jit_solution(2453588384706123003)
XLA Ops:
  0.0 31.3 %shard_map.55 = bf16[4,1024]{1,0:T(4,128)(2,1)} custom-call(bf16[4,4,512]{2,1,0:T(4,128)(2,1)} %q_ref.1, s32[4,4,32]{2,1,0:T(4,128)} %i_ref.1, bf16[4,8,256]{2,1,0:T(8,128)(2,1)} %fk_ref.1, bf16[4,1024,256]{2,1,0:T(8,128)(2,1)} %sk_ref.1, bf16[8192,1024]{1,0:T(8,128)(2,1)} %v_ref.1), custom_call_target="tpu_custom_call" | custom-call | tf_op jit(solution)/shard_map/pallas_call | solution.py:380
  31.3 1.3 %copy.7 = bf16[4,1024]{1,0:T(4,128)(2,1)} copy(bf16[4,1024]{1,0:T(4,128)(2,1)} %shard_map.55) | data formatting | bytes 16384

commit v3 on v2

--- a/solution.py
+++ b/solution.py
@@ -64,6 +64,8 @@
     k_recv,
     i_send,
     i_recv,
+    r_send,
+    r_recv,
     g_send,
     g_recv,
     q_send,
@@ -82,25 +84,31 @@
     rows, width = v_ref.shape
     t_me, b_me = lax.axis_index("table"), lax.axis_index("batch")
     dev_me = t_me * nb + b_me
+    core_me = lax.rem(t_me, 2)
     head_me = lax.rem(t_me, heads)
     group_me = lax.div(t_me, heads) * nb + b_me
     slot_me = head_me * groups + group_me
 
+    def flips(x, count):
+        bits = [(x // 2**i) % 2 for i in range(log2(count))]
+        return [
+            x + sum((1 - 2 * bit) * 2**i for i, bit in enumerate(bits) if mask >> i & 1)
+            for mask in range(count)
+        ]
+
+    t_flips, b_flips = flips(t_me, nt), flips(b_me, nb)
+    t_heads = [lax.rem(t, heads) for t in t_flips]
+    t_slots = [h * groups + lax.div(t, heads) * nb for t, h in zip(t_flips, t_heads)]
+    masks = sorted(
+        ((mt, mb) for mt in range(nt) for mb in range(nb) if mt or mb),
+        key=lambda m: (m[1] + bin(m[0] >> 1).count("1"), m),
+        reverse=True,
+    )
+
     def others(body, stride=1):
-        def visit(shift, first):
-            t = lax.rem(t_me + shift * stride, nt)
-            head = lax.rem(t, heads)
-            start = head * groups + lax.div(t, heads) * nb
-            for k in range(first, nb):
-                b = lax.rem(b_me + k, nb)
-                body(start + b, (t, b), head)
-
-        def step(shift, carry):
-            visit(shift, 0)
-            return carry
-
-        visit(0, 1)
-        lax.fori_loop(1, nt // stride, step, 0)
+        for mt, mb in masks:
+            if mt % stride == 0:
+                body(t_slots[mt] + b_flips[mb], (t_flips[mt], b_flips[mb]), t_heads[mt])
 
     def drain(ref, sem):
         pltpu.make_async_copy(ref, ref, sem).wait()
@@ -303,7 +311,6 @@
         copy.wait()
 
     piece = width // chunks
-    core_me = lax.rem(t_me, 2)
     half_slot = lax.div(head_me, 2) * groups + group_me
 
     def pass_on(c):
@@ -417,6 +424,8 @@
             dma,
             dma,
             dma,
+            dma,
+            dma,
             dma((chunks,)),
             dma((chunks,)),
             dma((chunks,)),

time: 32.9 us -> 32 us (0.973)
  Pallas kernels: 31.3 us -> 30.4 us
    pallas_call x1, Pallas kernels: 31.3 us -> 30.4 us  [shards(): pl.pallas_call(functools.partial(kernel, (nt, nb, heads, seqs, top, chunk...]
where the time goes in v3:
time: 32 us; the launch traced here: 31.7 us
  Pallas kernels  30.4 us (95%)
  local copies, waits for them, and re-layouts  1.3 us (4%)
    pallas_call x1, Pallas kernels, shards(): pl.pallas_call(functools.partial(kernel, (nt, nb, heads, seqs, top, chunk...  30.4 us
    unnamed x1, local copies, waits for them, and re-layouts  1.3 us

profile of v3, /device:TPU:0, one launch (start us, length us, event | category | flops | bytes accessed | tf_op | source)
XLA Modules:
  0.0 31.7 jit_solution(17420246115100046604)
XLA Ops:
  0.0 30.4 %shard_map.55 = bf16[4,1024]{1,0:T(4,128)(2,1)} custom-call(bf16[4,4,512]{2,1,0:T(4,128)(2,1)} %q_ref.1, s32[4,4,32]{2,1,0:T(4,128)} %i_ref.1, bf16[4,8,256]{2,1,0:T(8,128)(2,1)} %fk_ref.1, bf16[4,1024,256]{2,1,0:T(8,128)(2,1)} %sk_ref.1, bf16[8192,1024]{1,0:T(8,128)(2,1)} %v_ref.1), custom_call_target="tpu_custom_call" | custom-call | tf_op jit(solution)/shard_map/pallas_call | solution.py:387
  30.4 1.3 %copy.7 = bf16[4,1024]{1,0:T(4,128)(2,1)} copy(bf16[4,1024]{1,0:T(4,128)(2,1)} %shard_map.55) | data formatting | bytes 16384

commit v4 on v3

--- a/solution.py
+++ b/solution.py
@@ -113,6 +113,12 @@
     def drain(ref, sem):
         pltpu.make_async_copy(ref, ref, sem).wait()
 
+    barrier = pltpu.get_barrier_semaphore()
+    others(
+        lambda slot, where, head: pl.semaphore_signal(
+            barrier, inc=1, device_id=where, device_id_type=MESH
+        )
+    )
     k2_copy = pltpu.make_async_copy(sk_ref.at[head_me], k2buf, k2_sem)
     k2_copy.start()
     block = rows // pieces
@@ -125,12 +131,6 @@
     for copy in v_copies:
         copy.start()
 
-    barrier = pltpu.get_barrier_semaphore()
-    others(
-        lambda slot, where, head: pl.semaphore_signal(
-            barrier, inc=1, device_id=where, device_id_type=MESH
-        )
-    )
     for h in range(heads):
         for s in range(seqs):
             icomp[pl.ds(s, 1), pl.ds(h * top, top)] = i_ref[s, pl.ds(h, 1), :]
@@ -162,10 +162,6 @@
             device_id_type=MESH,
         ).start()
 
-    for j in range(1, heads):
-        send_q(j)
-        send_group_ids(j)
-
     def send_keys(slot, where, head):
         pltpu.make_async_remote_copy(
             src_ref=fk_ref.at[head],
@@ -187,6 +183,9 @@
         ).start()
 
     others(send_keys)
+    for j in range(1, heads):
+        send_q(j)
+        send_group_ids(j)
     others(send_ids)
 
     drain(qslot.at[pl.ds(0, heads - 1)], q_recv)
@@ -287,10 +286,11 @@
         wfin[pl.ds(j * span, span), :] = total
 
     pitch = all_seqs + 8
+    burst = min(all_seqs, LANES)
 
     def spread(step, carry):
-        for u in range(32):
-            s = step * 32 + u
+        for u in range(burst):
+            s = step * burst + u
             left = high_hot(s, wfin[pl.ds(s, 1), :])
             right = lows[s] if early else low_hot(s)
             wacc[pl.ds(s, high_count, stride=pitch), :] = lax.dot_general(
@@ -298,7 +298,7 @@
             )
         return carry
 
-    lax.fori_loop(0, all_seqs // 32, spread, 0)
+    lax.fori_loop(0, all_seqs // burst, spread, 0)
 
     def narrow(step, carry):
         wb[:, pl.ds(pl.multiple_of(step * LANES, LANES), LANES)] = wacc[

time: 32 us -> 31.6 us (0.988)
  Pallas kernels: 30.4 us -> 30 us
    pallas_call x1, Pallas kernels: 30.4 us -> 30 us  [shards(): pl.pallas_call(functools.partial(kernel, (nt, nb, heads, seqs, top, chunk...]
where the time goes in v4:
time: 31.6 us; the launch traced here: 31.3 us
  Pallas kernels  30 us (95%)
  local copies, waits for them, and re-layouts  1.3 us (4%)
    pallas_call x1, Pallas kernels, shards(): pl.pallas_call(functools.partial(kernel, (nt, nb, heads, seqs, top, chunk...  30 us
    unnamed x1, local copies, waits for them, and re-layouts  1.3 us

profile of v4, /device:TPU:0, one launch (start us, length us, event | category | flops | bytes accessed | tf_op | source)
XLA Modules:
  0.0 31.3 jit_solution(7078730567986581043)
XLA Ops:
  0.0 30.0 %shard_map.55 = bf16[4,1024]{1,0:T(4,128)(2,1)} custom-call(bf16[4,4,512]{2,1,0:T(4,128)(2,1)} %q_ref.1, s32[4,4,32]{2,1,0:T(4,128)} %i_ref.1, bf16[4,8,256]{2,1,0:T(8,128)(2,1)} %fk_ref.1, bf16[4,1024,256]{2,1,0:T(8,128)(2,1)} %sk_ref.1, bf16[8192,1024]{1,0:T(8,128)(2,1)} %v_ref.1), custom_call_target="tpu_custom_call" | custom-call | tf_op jit(solution)/shard_map/pallas_call | solution.py:387
  30.0 1.3 %copy.7 = bf16[4,1024]{1,0:T(4,128)(2,1)} copy(bf16[4,1024]{1,0:T(4,128)(2,1)} %shard_map.55) | data formatting | bytes 16384
